TPU v7x, 16 devices: a whole 2x2x2 slice. The times are simulated.
16 devices in a mesh: col: 2 (over z), row: 8 (over y, x, core).
Axes of the slice: x: 2, y: 2, z: 2, core: 2. Of those that a mesh axis runs over, the one named last changes fastest.
Arguments:
- vel_u: float32 [41, 1024, 256], P(None, 'row', 'col')
- vel_v: float32 [41, 1024, 256], P(None, 'row', 'col')
- temperature: float32 [41, 1024, 256], P(None, 'row', 'col')
- salinity: float32 [41, 1024, 256], P(None, 'row', 'col')
- sea_level: float32 [1024, 256], P('row', 'col')
- trans_u: float32 [1024, 256], P('row', 'col')
- trans_v: float32 [1024, 256], P('row', 'col')
- col_depth: float32 [1024, 256], P('row', 'col')
- kmt_levels: int32 [1024, 256], P('row', 'col')
Outputs:
- output 1: float32 [1024, 256], P('row', 'col')
- output 2: float32 [1024, 256], P('row', 'col')
- output 3: float32 [1024, 256], P('row', 'col')
- output 4: float32 [41, 1024, 256], P(None, 'row', 'col')
- output 5: float32 [41, 1024, 256], P(None, 'row', 'col')
- output 6: float32 [41, 1024, 256], P(None, 'row', 'col')
- output 7: float32 [41, 1024, 256], P(None, 'row', 'col')
All inputs are finite; a program needn't handle non-finite values.
Results may differ from a plain program's by a relative error of at most 0.001.
Values sent between devices are 32-bit elements.
A program may use at most 1 GiB of HBM per device.

v0:
```python
import jax
import jax.numpy as jnp
from jax import lax
from jax.sharding import PartitionSpec as P

SUBCYCLES = 30
ADV_COURANT = 0.25
WAVE_COURANT = 0.5
VISC_NUM = 4.0
DIFF_NUM = 1.0
ALPHA_T = 0.3
BETA_S = 0.6


def column_solve(wet_mask, diffusivity, rhs_list):
    link_mask = wet_mask[:-1] * wet_mask[1:]
    zero_level = jnp.zeros_like(wet_mask[:1])
    upper_band = diffusivity * jnp.concatenate([link_mask, zero_level], axis=0)
    lower_band = diffusivity * jnp.concatenate([zero_level, link_mask], axis=0)
    diag_band = 1.0 + upper_band + lower_band

    def forward(state_in, level_in):
        c_prev, d_prev = state_in
        up_k, lo_k, dg_k, rhs_k = level_in
        pivot = dg_k - lo_k * c_prev
        c_ratio = up_k / pivot
        d_new = tuple((r + lo_k * p) / pivot for r, p in zip(rhs_k, d_prev))
        return (c_ratio, d_new), (c_ratio, d_new)

    def backward(x_next, level_in):
        c_k, d_k = level_in
        x_new = tuple(d + c_k * x for d, x in zip(d_k, x_next))
        return x_new, x_new

    zero_plane = jnp.zeros_like(wet_mask[0])
    start_state = (zero_plane, tuple(zero_plane for _ in rhs_list))
    _, (c_all, d_all) = lax.scan(forward, start_state, (upper_band, lower_band, diag_band, tuple(rhs_list)))
    _, x_all = lax.scan(backward, tuple(zero_plane for _ in rhs_list), (c_all, d_all), reverse=True)
    return x_all


def upwind_div(u_pad, v_pad, tracer_pad, face_u, face_v):
    u_face = u_pad[:, 1:-1, :-1]
    flux_e = face_u[:, 1:-1, :] * (jnp.maximum(u_face, 0.0) * tracer_pad[:, 1:-1, :-1] + jnp.minimum(u_face, 0.0) * tracer_pad[:, 1:-1, 1:])
    v_face = v_pad[:, :-1, 1:-1]
    flux_n = face_v[:, :, 1:-1] * (jnp.maximum(v_face, 0.0) * tracer_pad[:, :-1, 1:-1] + jnp.minimum(v_face, 0.0) * tracer_pad[:, 1:, 1:-1])
    return flux_e[:, :, 1:] - flux_e[:, :, :-1] + flux_n[:, 1:, :] - flux_n[:, :-1, :]


def baroclinic(u_pad, v_pad, t_pad, s_pad, kmt_pad, depth_pad):
    level_idx = jnp.arange(u_pad.shape[0], dtype=jnp.int32)[:, None, None]
    cell_p = (level_idx < kmt_pad[None]).astype(jnp.float32)
    kmin_u = jnp.minimum(kmt_pad[:, :-1], kmt_pad[:, 1:])
    kmin_v = jnp.minimum(kmt_pad[:-1, :], kmt_pad[1:, :])
    face_u = (level_idx < kmin_u[None]).astype(jnp.float32)
    face_v = (level_idx < kmin_v[None]).astype(jnp.float32)
    thickness = depth_pad / jnp.maximum(kmt_pad, 1).astype(jnp.float32)
    density = (BETA_S * s_pad - ALPHA_T * t_pad) * cell_p
    pressure = (jnp.cumsum(density, axis=0) - 0.5 * density) * thickness[None]
    u_c = u_pad[:, 1:-1, 1:-1]
    v_c = v_pad[:, 1:-1, 1:-1]
    p_c = pressure[:, 1:-1, 1:-1]
    mask_u = face_u[:, 1:-1, 1:]
    mask_v = face_v[:, 1:, 1:-1]
    cell_c = cell_p[:, 1:-1, 1:-1]
    v_at_u = 0.25 * (v_c + v_pad[:, 1:-1, 2:] + v_pad[:, :-2, 1:-1] + v_pad[:, :-2, 2:])
    u_at_v = 0.25 * (u_c + u_pad[:, 1:-1, :-2] + u_pad[:, 2:, 1:-1] + u_pad[:, 2:, :-2])
    tend_u = mask_u * (p_c - pressure[:, 1:-1, 2:] - 0.5 * (u_c * (u_pad[:, 1:-1, 2:] - u_pad[:, 1:-1, :-2]) + v_at_u * (u_pad[:, 2:, 1:-1] - u_pad[:, :-2, 1:-1])))
    tend_v = mask_v * (p_c - pressure[:, 2:, 1:-1] - 0.5 * (u_at_v * (v_pad[:, 1:-1, 2:] - v_pad[:, 1:-1, :-2]) + v_c * (v_pad[:, 2:, 1:-1] - v_pad[:, :-2, 1:-1])))
    new_u = column_solve(mask_u, VISC_NUM, (mask_u * (u_c + ADV_COURANT * tend_u),))[0]
    new_v = column_solve(mask_v, VISC_NUM, (mask_v * (v_c + ADV_COURANT * tend_v),))[0]
    pred_t = cell_c * (t_pad[:, 1:-1, 1:-1] - ADV_COURANT * upwind_div(u_pad, v_pad, t_pad, face_u, face_v))
    pred_s = cell_c * (s_pad[:, 1:-1, 1:-1] - ADV_COURANT * upwind_div(u_pad, v_pad, s_pad, face_u, face_v))
    new_t, new_s = column_solve(cell_c, DIFF_NUM, (pred_t, pred_s))
    count_u = kmin_u[1:-1, 1:]
    count_v = kmin_v[1:, 1:-1]
    wet_u = (count_u > 0).astype(jnp.float32)
    wet_v = (count_v > 0).astype(jnp.float32)
    wet_c = (kmt_pad[1:-1, 1:-1] > 0).astype(jnp.float32)
    inv_u = 1.0 / jnp.maximum(count_u, 1).astype(jnp.float32)
    inv_v = 1.0 / jnp.maximum(count_v, 1).astype(jnp.float32)
    depth_u = 0.5 * (depth_pad[1:-1, 1:-1] + depth_pad[1:-1, 2:]) * wet_u
    depth_v = 0.5 * (depth_pad[1:-1, 1:-1] + depth_pad[2:, 1:-1]) * wet_v
    force_u = depth_u * inv_u * jnp.sum(tend_u, axis=0)
    force_v = depth_v * inv_v * jnp.sum(tend_v, axis=0)
    base_u = new_u - mask_u * (inv_u * jnp.sum(new_u, axis=0))[None]
    base_v = new_v - mask_v * (inv_v * jnp.sum(new_v, axis=0))[None]
    return (base_u, base_v, mask_u, mask_v, new_t, new_s, force_u, force_v, depth_u, depth_v, wet_u, wet_v, wet_c)


def sm_weights():
    frac_step = jnp.arange(1, SUBCYCLES + 1, dtype=jnp.float32) / (SUBCYCLES + 1)
    raw_shape = frac_step ** 2 * (1.0 - frac_step ** 4)
    return raw_shape / jnp.sum(raw_shape)


def finish(base_vel, face_mask, mean_flow, face_depth):
    return base_vel + face_mask * (mean_flow / jnp.where(face_depth > 0, face_depth, 1.0))[None]


def solution(mesh):
    col_count = mesh.shape['col']
    row_count = mesh.shape['row']
    to_east = [(c, (c + 1) % col_count) for c in range(col_count)]
    to_west = [((c + 1) % col_count, c) for c in range(col_count)]
    to_north = [(r, r + 1) for r in range(row_count - 1)]
    to_south = [(r + 1, r) for r in range(row_count - 1)]

    def halo_pad(field_in):
        from_west = lax.ppermute(field_in[..., -1:], 'col', to_east)
        from_east = lax.ppermute(field_in[..., :1], 'col', to_west)
        wide_pad = jnp.concatenate([from_west, field_in, from_east], axis=-1)
        from_south = lax.ppermute(wide_pad[..., -1:, :], 'row', to_north)
        from_north = lax.ppermute(wide_pad[..., :1, :], 'row', to_south)
        return jnp.concatenate([from_south, wide_pad, from_north], axis=-2)

    def ocean_step(vel_u, vel_v, value_a11, salinity, sea_level, trans_u, trans_v, col_depth, kmt_levels):
        fields_pad = halo_pad(jnp.stack([vel_u, vel_v, value_a11, salinity]))
        kmt_pad = halo_pad(kmt_levels)
        depth_pad = halo_pad(col_depth)
        (base_u, base_v, mask_u, mask_v, new_t, new_s, force_u, force_v, depth_u, depth_v, wet_u, wet_v, wet_c) = baroclinic(fields_pad[0], fields_pad[1], fields_pad[2], fields_pad[3], kmt_pad, depth_pad)
        wave_u = WAVE_COURANT * depth_u
        wave_v = WAVE_COURANT * depth_v
        push_u = (ADV_COURANT / SUBCYCLES) * force_u
        push_v = (ADV_COURANT / SUBCYCLES) * force_v

        def subcycle(state_in, weight):
            level_now, flow_u, flow_v, mean_u, mean_v = state_in
            west_col = lax.ppermute(flow_u[:, -1:], 'col', to_east)
            south_row = lax.ppermute(flow_v[-1:, :], 'row', to_north)
            west_u = jnp.concatenate([west_col, flow_u[:, :-1]], axis=1)
            south_v = jnp.concatenate([south_row, flow_v[:-1]], axis=0)
            level_new = wet_c * (level_now - WAVE_COURANT * (flow_u - west_u + flow_v - south_v))
            east_col = lax.ppermute(level_new[:, :1], 'col', to_west)
            north_row = lax.ppermute(level_new[:1, :], 'row', to_south)
            east_level = jnp.concatenate([level_new[:, 1:], east_col], axis=1)
            north_level = jnp.concatenate([level_new[1:], north_row], axis=0)
            flow_u = wet_u * (flow_u - wave_u * (east_level - level_new) + push_u)
            flow_v = wet_v * (flow_v - wave_v * (north_level - level_new) + push_v)
            return (level_new, flow_u, flow_v, mean_u + weight * flow_u, mean_v + weight * flow_v), None

        start_state = (wet_c * sea_level, wet_u * trans_u, wet_v * trans_v, jnp.zeros_like(trans_u), jnp.zeros_like(trans_v))
        final_state, _ = lax.scan(subcycle, start_state, sm_weights())
        level_new, flow_u, flow_v, mean_u, mean_v = final_state
        return (level_new, flow_u, flow_v, finish(base_u, mask_u, mean_u, depth_u), finish(base_v, mask_v, mean_v, depth_v), new_t, new_s)

    spec_3d = P(None, 'row', 'col')
    spec_2d = P('row', 'col')
    return jax.shard_map(ocean_step, mesh=mesh, in_specs=(spec_3d, spec_3d, spec_3d, spec_3d, spec_2d, spec_2d, spec_2d, spec_2d, spec_2d), out_specs=(spec_2d, spec_2d, spec_2d, spec_3d, spec_3d, spec_3d, spec_3d), check_vma=False)
```

profile of v0, /device:TPU:12, one launch (start us, length us, event | category | flops | bytes accessed | tf_op | source)
XLA Modules:
  0.0 1160.3 jit_solution(12288387120425041613)
XLA Ops:
  8.3 5.0 pad_maximum_fusion.1
  13.3 8.8 fusion.86
  27.9 4.0 collective-permute-start.7
  34.1 6.2 copy.17
  40.3 6.2 copy.16
  69.3 5.8 copy.19
  75.1 6.4 copy.18
  85.0 4.4 collective-permute-start.12
  97.2 20.5 %pad_maximum_fusion = f32[4,41,130,130]{3,2,1,0:T(8,128)} fusion(f32[4,41,1,130]{3,2,1,0:T(1,128)S(1)} %collective-permute-done.12, f32[4,41,128,1]{3,2,1,0:T(8,128)S(1)} %bitcast.191, f32[1,41,128,128]{3,2,1,0:T(8,128)S(1)} %bitcast.196, f32[1,41,128,128]{3,2,1,0:T(8,128)S(1)} %bitcast.199, f32[1,41,128,128]{3,2,1,0:T(8,128)S(1)} %bitcast.202, ...), kind=kLoop, calls=%fused_computation.58 | loop fusion | flops 19401200 | bytes 22172800 | tf_op jit(solution)/shard_map/concatenate | solution.py:115
  117.7 14.3 %slice_bitcast_fusion.3 = (f32[41,130,130]{2,1,0:T(8,128)}, f32[41,130,130]{2,1,0:T(8,128)}, f32[41,130,130]{2,1,0:T(8,128)S(1)}, f32[41,130,130]{2,1,0:T(8,128)}) fusion(f32[4,41,130,130]{3,2,1,0:T(8,128)} %pad_maximum_fusion), kind=kLoop, calls=%fused_computation.63 | loop fusion | bytes 22172800 | tf_op jit(solution)/shard_map/squeeze | solution.py:121
  132.0 11.4 subtract_multiply_fusion
  143.4 22.5 %add_multiply_fusion.1 = (f32[41,128,128]{2,1,0:T(8,128)}, f32[41,128,128]{2,1,0:T(8,128)}) fusion(f32[41,130,130]{2,1,0:T(8,128)S(1)} %get-tuple-element.1014, f32[41,130,129]{2,1,0:T(8,128)} %copy-done.1, f32[41,130,130]{2,1,0:T(8,128)} %get-tuple-element.1013, f32[41,130,130]{2,1,0:T(8,128)} %subtract_multiply_fusion), kind=kLoop, calls=%fused_computation.131 | loop fusion | flops 10747904 | bytes 37617664 | tf_op jit(solution)/shard_map/mul | solution.py:70
  165.8 22.3 %add_multiply_fusion = (f32[41,128,128]{2,1,0:T(8,128)}, f32[41,128,128]{2,1,0:T(8,128)}) fusion(f32[41,129,130]{2,1,0:T(8,128)} %copy-done.2, f32[41,130,130]{2,1,0:T(8,128)} %get-tuple-element.1013, f32[41,130,130]{2,1,0:T(8,128)S(1)} %get-tuple-element.1014, f32[41,130,130]{2,1,0:T(8,128)} %subtract_multiply_fusion), kind=kLoop, calls=%fused_computation.126 | loop fusion | flops 10747904 | bytes 37617664 | tf_op jit(solution)/shard_map/mul | solution.py:71
  188.1 17.1 %fusion.31 = (f32[41,129,128]{2,1,0:T(8,128)}, f32[41,129,128]{2,1,0:T(8,128)}) fusion(f32[41,130,130]{2,1,0:T(8,128)} %get-tuple-element.1012, f32[41,129,130]{2,1,0:T(8,128)} %copy-done.2, f32[41,130,130]{2,1,0:T(8,128)} %get-tuple-element.1013, f32[41,130,130]{2,1,0:T(8,128)} %get-tuple-element.1015), kind=kLoop, calls=%fused_computation.84 | loop fusion | flops 6769920 | bytes 21663744 | tf_op jit(solution)/shard_map/mul | solution.py:46
  205.2 17.3 %fusion.27 = (f32[41,128,129]{2,1,0:T(8,128)}, f32[41,128,129]{2,1,0:T(8,128)}) fusion(f32[41,130,130]{2,1,0:T(8,128)} %get-tuple-element.1012, f32[41,130,129]{2,1,0:T(8,128)} %copy-done.1, f32[41,130,130]{2,1,0:T(8,128)S(1)} %get-tuple-element.1014, f32[41,130,130]{2,1,0:T(8,128)} %get-tuple-element.1015), kind=kLoop, calls=%fused_computation.74 | loop fusion | flops 6769920 | bytes 21663744 | tf_op jit(solution)/shard_map/mul | solution.py:44
  226.2 67.1 %while.130 = (s32[]{:T(128)}, f32[128,128]{1,0:T(8,128)S(1)}, f32[128,128]{1,0:T(8,128)S(1)}, f32[41,128,128]{2,1,0:T(8,128)}, f32[41,128,128]{2,1,0:T(8,128)}, ...) while((s32[]{:T(128)}, f32[128,128]{1,0:T(8,128)S(1)}, ...), condition=%wide.region_7.8_spmd.clone, body=%wide.region_6.7_spmd.clone.sunk | while | flops 131075 | bytes 655491 | solution.py:37
  295.1 63.2 %while.131 = (s32[]{:T(128)}, f32[128,128]{1,0:T(8,128)S(1)}, f32[41,128,128]{2,1,0:T(8,128)}, f32[41,128,128]{2,1,0:T(8,128)}, f32[41,128,128]{2,1,0:T(8,128)}, /*index=5*/s32[]{:T(128)}, s32[]{:T(128)}, s32[]{:T(128)}) while((s32[]{:T(128)}, f32[128,128]{1,0:T(8,128)S(1)}, f32[41,128,128]{2,1,0:T(8,128)}, ...), condition=%wide.region_9.10_spmd.clone, body=%wide.region_8.9_spmd.clone.sunk | while | flops 49156 | bytes 327799 | solution.py:38
  362.0 66.9 %while.132 = (s32[]{:T(128)}, f32[128,128]{1,0:T(8,128)S(1)}, f32[128,128]{1,0:T(8,128)S(1)}, f32[41,128,128]{2,1,0:T(8,128)}, f32[41,128,128]{2,1,0:T(8,128)}, ...) while((s32[]{:T(128)}, f32[128,128]{1,0:T(8,128)S(1)}, ...), condition=%wide.region_12.13_spmd.clone, body=%wide.region_11.12_spmd.clone.sunk | while | flops 131075 | bytes 655491 | solution.py:37
  430.8 63.2 %while.133 = (s32[]{:T(128)}, f32[128,128]{1,0:T(8,128)S(1)}, f32[41,128,128]{2,1,0:T(8,128)}, f32[41,128,128]{2,1,0:T(8,128)}, f32[41,128,128]{2,1,0:T(8,128)}, /*index=5*/s32[]{:T(128)}, s32[]{:T(128)}, s32[]{:T(128)}) while((s32[]{:T(128)}, f32[128,128]{1,0:T(8,128)S(1)}, f32[41,128,128]{2,1,0:T(8,128)}, ...), condition=%wide.region_14.15_spmd.clone, body=%wide.region_13.14_spmd.clone.sunk | while | flops 49156 | bytes 327799 | solution.py:38
  503.0 426.9 %while.129 = (s32[]{:T(128)}, f32[128,128]{1,0:T(8,128)S(1)}, f32[128,128]{1,0:T(8,128)S(1)}, f32[128,128]{1,0:T(8,128)S(1)}, f32[128,128]{1,0:T(8,128)S(1)}, /*...) while((s32[]{:T(128)}, f32[128,128]{1,0:T(8,128)S(1)}, ...), condition=%wide.region_5.6_spmd.clone, body=%wide.region_4.5_spmd.clone.sunk | while | flops 425987 | bytes 1844567 | solution.py:143
  930.0 18.1 %fusion.36 = (f32[41,128,128]{2,1,0:T(8,128)}, f32[41,128,128]{2,1,0:T(8,128)}) fusion(f32[41,129,128]{2,1,0:T(8,128)} %get-tuple-element.1018, f32[41,128,129]{2,1,0:T(8,128)} %get-tuple-element.1016, f32[41,130,130]{2,1,0:T(8,128)} %get-tuple-element.1012, f32[41,130,130]{2,1,0:T(8,128)} %copy-done.3, f32[41,129,128]{2,1,0:T(8,128)} %get-tuple-element.1019, ...), kind=kLoop, calls=%fused_computation.93 | loop fusion | flops 8060928 | bytes 34930688 | tf_op jit(solution)/shard_map/mul | solution.py:73
  952.2 128.0 %while.134 = (s32[]{:T(128)}, f32[128,128]{1,0:T(8,128)S(1)}, f32[128,128]{1,0:T(8,128)S(1)}, f32[128,128]{1,0:T(8,128)S(1)}, f32[41,128,128]{2,1,0:T(8,128)S(1)...) while((s32[]{:T(128)}, f32[128,128]{1,0:T(8,128)S(1)}, ...), condition=%wide.region_17.18_spmd.clone, body=%wide.region_16.17_spmd.clone.sunk | while | flops 196611 | bytes 1114272 | solution.py:37
  1085.3 65.4 %while.135 = (s32[]{:T(128)}, f32[128,128]{1,0:T(8,128)S(1)}, f32[128,128]{1,0:T(8,128)S(1)}, f32[41,128,128]{2,1,0:T(8,128)}, f32[41,128,128]{2,1,0:T(8,128)}, ...) while((s32[]{:T(128)}, f32[128,128]{1,0:T(8,128)S(1)}, ...), condition=%wide.region_19.20_spmd.clone, body=%wide.region_18.19_spmd.clone.sunk | while | flops 98308 | bytes 589967 | solution.py:38
  1150.7 9.1 multiply_add_fusion
  (918 shorter events, 957.4 us)
Async XLA Ops:
  1.6 21.7 %collective-permute-start.8 = (f32[128,1]{1,0:T(8,128)S(1)}, f32[128,1]{1,0:T(8,128)S(1)}, u32[]{:S(2)}, u32[]{:S(2)}) collective-permute-start(f32[128,1]{1,0:T(8,128)S(1)} %get-tuple-element.1045), channel_id=1, source_target_pairs={{8,0},{0,8},{9,1},{1,9},{10,2},{2,10},{11,3},{3,11},{12,4},{4,12},... | collective-permute-start | bytes 1544 | tf_op jit(solution)/shard_map/ppermute | solution.py:111
  2.1 21.3 %collective-permute-start.13 = (f32[128,1]{1,0:T(8,128)S(1)}, f32[128,1]{1,0:T(8,128)S(1)}, u32[]{:S(2)}, u32[]{:S(2)}) collective-permute-start(f32[128,1]{1,0:T(8,128)S(1)} %get-tuple-element.1044), channel_id=1, source_target_pairs={{0,8},{8,0},{1,9},{9,1},{2,10},{10,2},{3,11},{11,3},{4,12},{12,4},... | collective-permute-start | bytes 1544 | tf_op jit(solution)/shard_map/ppermute | solution.py:110
  4.7 23.1 %collective-permute-start.5 = (s32[128,1]{1,0:T(8,128)S(1)}, s32[128,1]{1,0:T(8,128)S(1)}, u32[]{:S(2)}, u32[]{:S(2)}) collective-permute-start(s32[128,1]{1,0:T(8,128)S(1)} %get-tuple-element.1043), channel_id=1, source_target_pairs={{8,0},{0,8},{9,1},{1,9},{10,2},{2,10},{11,3},{3,11},{12,4},{4,12},... | collective-permute-start | bytes 1544 | tf_op jit(solution)/shard_map/ppermute | solution.py:111
  5.2 22.7 %collective-permute-start.4 = (s32[128,1]{1,0:T(8,128)S(1)}, s32[128,1]{1,0:T(8,128)S(1)}, u32[]{:S(2)}, u32[]{:S(2)}) collective-permute-start(s32[128,1]{1,0:T(8,128)S(1)} %get-tuple-element.1042), channel_id=1, source_target_pairs={{0,8},{8,0},{1,9},{9,1},{2,10},{10,2},{3,11},{11,3},{4,12},{12,4},... | collective-permute-start | bytes 1544 | tf_op jit(solution)/shard_map/ppermute | solution.py:110
  23.5 23.5 %collective-permute-start.15 = (f32[1,130]{1,0:T(1,128)S(1)}, f32[1,130]{1,0:T(1,128)S(1)}, u32[]{:S(2)}, u32[]{:S(2)}) collective-permute-start(f32[1,130]{1,0:T(1,128)S(1)} %get-tuple-element.1036), channel_id=1, source_target_pairs={{1,0},{2,1},{3,2},{4,3},{5,4},{6,5},{7,6},{9,8},{10,9},{11,10},{12... | collective-permute-start | bytes 1568 | tf_op jit(solution)/shard_map/ppermute | solution.py:114
  25.4 23.2 %collective-permute-start.14 = (f32[1,130]{1,0:T(1,128)S(1)}, f32[1,130]{1,0:T(1,128)S(1)}, u32[]{:S(2)}, u32[]{:S(2)}) collective-permute-start(f32[1,130]{1,0:T(1,128)S(1)} %get-tuple-element.1035), channel_id=1, source_target_pairs={{0,1},{1,2},{2,3},{3,4},{4,5},{5,6},{6,7},{8,9},{9,10},{10,11},{11... | collective-permute-start | bytes 1568 | tf_op jit(solution)/shard_map/ppermute | solution.py:113
  27.9 20.7 %collective-permute-start.7 = (s32[1,130]{1,0:T(1,128)S(1)}, s32[1,130]{1,0:T(1,128)S(1)}, u32[]{:S(2)}, u32[]{:S(2)}) collective-permute-start(s32[1,130]{1,0:T(1,128)S(1)} %get-tuple-element.1034), channel_id=1, source_target_pairs={{1,0},{2,1},{3,2},{4,3},{5,4},{6,5},{7,6},{9,8},{10,9},{11,10},{12... | collective-permute-start | bytes 1568 | tf_op jit(solution)/shard_map/ppermute | solution.py:114
  32.0 16.6 %collective-permute-start.6 = (s32[1,130]{1,0:T(1,128)S(1)}, s32[1,130]{1,0:T(1,128)S(1)}, u32[]{:S(2)}, u32[]{:S(2)}) collective-permute-start(s32[1,130]{1,0:T(1,128)S(1)} %get-tuple-element.1033), channel_id=1, source_target_pairs={{0,1},{1,2},{2,3},{3,4},{4,5},{5,6},{6,7},{8,9},{9,10},{10,11},{11... | collective-permute-start | bytes 1568 | tf_op jit(solution)/shard_map/ppermute | solution.py:113
  46.5 22.8 %collective-permute-start.10 = (f32[4,41,128,1]{2,0,3,1:T(4,128)S(1)}, f32[4,41,128,1]{2,0,3,1:T(4,128)S(1)}, u32[]{:S(2)}, u32[]{:S(2)}) collective-permute-start(f32[4,41,128,1]{2,0,3,1:T(4,128)S(1)} %copy.17), channel_id=1, source_target_pairs={{8,0},{0,8},{9,1},{1,9},{10,2},{2,10},{11,3},{3,11},{12,4},{4,12},... | collective-permute-start | bytes 251912 | tf_op jit(solution)/shard_map/ppermute | solution.py:111
  47.0 28.1 %collective-permute-start.9 = (f32[4,41,128,1]{2,0,3,1:T(4,128)S(1)}, f32[4,41,128,1]{2,0,3,1:T(4,128)}, u32[]{:S(2)}, u32[]{:S(2)}) collective-permute-start(f32[4,41,128,1]{2,0,3,1:T(4,128)S(1)} %copy.16), channel_id=1, source_target_pairs={{0,8},{8,0},{1,9},{9,1},{2,10},{10,2},{3,11},{11,3},{4,12},{12,4},... | collective-permute-start | bytes 251912 | tf_op jit(solution)/shard_map/ppermute | solution.py:110
  85.0 8.5 collective-permute-start.12
  89.3 7.8 collective-permute-start.11
  503.6 5.8 collective-permute-start.1
  518.4 5.8 collective-permute-start.1
  532.0 5.8 collective-permute-start.1
  546.8 5.8 collective-permute-start.1
  560.5 5.8 collective-permute-start.1
  588.9 5.8 collective-permute-start.1
  603.7 5.8 collective-permute-start.1
  617.4 5.8 collective-permute-start.1
  632.2 5.8 collective-permute-start.1
  645.9 5.8 collective-permute-start.1
  660.7 5.8 collective-permute-start.1
  674.3 5.8 collective-permute-start.1
  (144 other events, 918.9 us)
where the time goes:
time: 1180 us; the launch traced here: 1160 us
  other arithmetic  657 us (56%)
  waiting for transfers between devices  204 us (17%)
  starting transfers between devices  201 us (17%)
  local copies, waits for them, and re-layouts  95.5 us (8%)
    dynamic_update_slice x287, other arithmetic, column_solve(): lax.scan(forward, start_state, (upper_band, lower_band, diag_band, tuple(...  454 us
    ppermute x30, waiting for transfers between devices, subcycle(): east_col = lax.ppermute(level_new[:, :1], 'col', to_west)  82.4 us
    ppermute x30, waiting for transfers between devices, subcycle(): south_row = lax.ppermute(flow_v[-1:, :], 'row', to_north)  76 us
    ppermute x30, starting transfers between devices, subcycle(): north_row = lax.ppermute(level_new[:1, :], 'row', to_south)  57.6 us
    ppermute x30, starting transfers between devices, subcycle(): south_row = lax.ppermute(flow_v[-1:, :], 'row', to_north)  57.3 us
    ppermute x30, waiting for transfers between devices, subcycle(): west_col = lax.ppermute(flow_u[:, -1:], 'col', to_east)  40 us
    ppermute x30, starting transfers between devices, subcycle(): east_col = lax.ppermute(level_new[:, :1], 'col', to_west)  31.5 us
    ppermute x30, starting transfers between devices, subcycle(): west_col = lax.ppermute(flow_u[:, -1:], 'col', to_east)  30.7 us
  transfers between devices with their start and end apart: 132, of which 106 were waited for; matrix products, arithmetic and copies ran while one was open for 6% of the time, Pallas kernels for 0%

commit v1 on v0

v1 whole, which is shorter than its diff:
```python
import functools

import jax
import jax.numpy as jnp
import numpy as np
from jax import lax
from jax.experimental import pallas as pl
from jax.experimental.pallas import tpu as pltpu
from jax.sharding import PartitionSpec as P

SUBCYCLES = 30
ADV_COURANT = 0.25
WAVE_COURANT = 0.5
VISC_NUM = 4.0
DIFF_NUM = 1.0
ALPHA_T = 0.3
BETA_S = 0.6

MESH = pl.DeviceIdType.MESH
f32 = jnp.float32

LV = 41
NB = 128
PAD = 8
NP = NB + 2 * PAD
HW = 32
NW = NB + 2 * HW
NWP = NW + 2 * PAD
R = 32
CH = NB // R
F_STRIDE = 2 * LV
L_KMT = 4 * F_STRIDE
L_DEP = L_KMT + 2


def solver_tables():
    out = np.zeros((8, 128), np.float64)
    for base, a in ((0, VISC_NUM), (3, DIFF_NUM)):
        c = 0.0
        for k in range(LV):
            lo = a if k > 0 else 0.0
            inner = 1.0 / (1.0 + a + lo - lo * c)
            last = 1.0 / (1.0 + lo - lo * c)
            out[base, k] = inner
            out[base + 1, k] = last
            c = a * inner
            out[base + 2, k] = c
    s = np.arange(1, SUBCYCLES + 1) / (SUBCYCLES + 1)
    w = s ** 2 * (1.0 - s ** 4)
    out[6, :SUBCYCLES] = w / w.sum()
    return out.astype(np.float32)


def lanes(rows):
    return lax.broadcasted_iota(jnp.int32, (rows, NB), 1)


def roll(x, s):
    return pltpu.roll(x, s, 1)


def east(x, halo, l0):
    return roll(jnp.where(l0, halo, x), NB - 1)


def west(x, halo, l127):
    return roll(jnp.where(l127, halo, x), 1)


def halo_lanes(ref, lane, rows):
    return roll(ref[lane // NB, rows, :], NB - 1 - lane % NB)


def pack_items(tile):
    items = []
    for f in range(4):
        for k in range(LV):
            lane = f * F_STRIDE + 2 * k
            if lane // NB == tile:
                items.append((f, k, lane % NB))
    return items


def pair(a, b):
    return jnp.where(lanes(a.shape[0]) < 64, roll(a, 32), roll(b, 96))


def unpair(p):
    l = lanes(p.shape[0])
    ok = (l < HW) | (l >= NB - HW)
    return jnp.where(ok, roll(p, 96), 0.0), jnp.where(ok, roll(p, 32), 0.0)


def momentum_kernel(nrow, tab, u_h, v_h, t_h, s_h, eta_r, tu_r, tv_r, dep_r, kmt_r,
                    rowh, pko, kdo, u2, v2, corr, eta_o, tu_o, tv_o,
                    xb, pb, pk, pks, pz, pw, kd, wo, wx, wps, bt, mean,
                    lsem, ssem, rsem):
    col = lax.axis_index("col")
    row = lax.axis_index("row")
    oc = 1 - col
    has_n = row < nrow - 1
    has_s = row > 0

    for f, src in enumerate((u_h, v_h, t_h, s_h)):
        pltpu.make_async_copy(src, xb.at[f, :, pl.ds(PAD, NB), :], lsem.at[f]).start()

    def at_wall(edge, rows, wrows):
        @pl.when(edge)
        def _():
            kd[:, rows, :] = jnp.zeros((2, PAD, NB), f32)
            pk[:, rows, :] = jnp.zeros((3, PAD, NB), f32)
            wo[:, wrows, :] = jnp.zeros((6, HW, NB), f32)
            wx[:, wrows, :] = jnp.zeros((3, HW, NB), f32)

            def zero(k, c):
                for f in range(4):
                    xb[f, k, rows, :] = jnp.zeros((PAD, NB), f32)
                return c
            lax.fori_loop(0, LV, zero, 0)

    at_wall(jnp.logical_not(has_s), pl.ds(0, PAD), pl.ds(0, HW))
    at_wall(jnp.logical_not(has_n), pl.ds(PAD + NB, PAD), pl.ds(HW + NB, HW))

    bar = pltpu.get_barrier_semaphore()

    def greet(dev):
        pl.semaphore_signal(bar, inc=1, device_id=dev, device_id_type=MESH)

    greet({"col": oc, "row": row})

    @pl.when(has_n)
    def _():
        greet({"col": col, "row": row + 1})
        greet({"col": oc, "row": row + 1})

    @pl.when(has_s)
    def _():
        greet({"col": col, "row": row - 1})
        greet({"col": oc, "row": row - 1})

    kmf = kmt_r[...].astype(f32)
    dm = jnp.where(kmt_r[...] > 0, dep_r[...], 0.0)
    kd[0, pl.ds(PAD, NB), :] = kmf
    kd[1, pl.ds(PAD, NB), :] = dm
    own = pl.ds(HW, NB)
    wo[0, own, :] = eta_r[...]
    wo[1, own, :] = tu_r[...]
    wo[2, own, :] = tv_r[...]
    wo[3, own, :] = dm
    wps[0] = pair(eta_r[...], tu_r[...])
    wps[1] = pair(tv_r[...], dm)

    pl.semaphore_wait(bar, 1 + 2 * has_n.astype(jnp.int32) + 2 * has_s.astype(jnp.int32))

    class Group:
        def __init__(self, cond, dev):
            self.cond, self.dev, self.copies = cond, dev, {}

        def add(self, key, sem, src, dst):
            self.copies[key] = pltpu.make_async_remote_copy(
                src_ref=src, dst_ref=dst, send_sem=ssem.at[sem], recv_sem=rsem.at[sem],
                device_id=self.dev, device_id_type=MESH)

        def each(self, keys, what):
            def run():
                for key in keys:
                    what(self.copies[key])
            if self.cond is None:
                run()
            else:
                pl.when(self.cond)(run)

    g_c = Group(None, {"col": oc, "row": row})
    g_n = Group(has_n, {"col": col, "row": row + 1})
    g_s = Group(has_s, {"col": col, "row": row - 1})
    d_n = Group(has_n, {"col": oc, "row": row + 1})
    d_s = Group(has_s, {"col": oc, "row": row - 1})
    hi, lo = pl.ds(PAD + NB - 1, 1), pl.ds(PAD, 1)
    hs, hn = pl.ds(PAD - 1, 1), pl.ds(PAD + NB, 1)
    w_hi, w_lo = pl.ds(NB, HW), pl.ds(HW, HW)
    w_s, w_n = pl.ds(0, HW), pl.ds(HW + NB, HW)
    for t in range(3):
        g_c.add(("p", t), t, pks.at[t], pk.at[t, pl.ds(PAD, NB), :])
    g_c.add("w", 3, wps.at[pl.ds(0, 2)], wx.at[pl.ds(0, 2), own, :])
    g_c.add("f", 4, wps.at[pl.ds(2, 1)], wx.at[pl.ds(2, 1), own, :])
    for f in range(4):
        g_n.add(("x", f), 5 + f, xb.at[f, :, hi, :], xb.at[f, :, hs, :])
        g_s.add(("x", f), 9 + f, xb.at[f, :, lo, :], xb.at[f, :, hn, :])
    g_n.add("k", 13, kd.at[:, hi, :], kd.at[:, hs, :])
    g_s.add("k", 14, kd.at[:, lo, :], kd.at[:, hn, :])
    g_n.add("w", 15, wo.at[pl.ds(0, 4), w_hi, :], wo.at[pl.ds(0, 4), w_s, :])
    g_s.add("w", 16, wo.at[pl.ds(0, 4), w_lo, :], wo.at[pl.ds(0, 4), w_n, :])
    g_n.add("f", 17, wo.at[pl.ds(4, 2), w_hi, :], wo.at[pl.ds(4, 2), w_s, :])
    g_s.add("f", 18, wo.at[pl.ds(4, 2), w_lo, :], wo.at[pl.ds(4, 2), w_n, :])
    d_n.add("p", 19, pks.at[:, pl.ds(NB - 1, 1), :], pk.at[:, hs, :])
    d_s.add("p", 20, pks.at[:, pl.ds(0, 1), :], pk.at[:, hn, :])
    d_n.add("w", 21, wps.at[pl.ds(0, 2), pl.ds(NB - HW, HW), :], wx.at[pl.ds(0, 2), w_s, :])
    d_s.add("w", 22, wps.at[pl.ds(0, 2), pl.ds(0, HW), :], wx.at[pl.ds(0, 2), w_n, :])
    d_n.add("f", 23, wps.at[pl.ds(2, 1), pl.ds(NB - HW, HW), :], wx.at[pl.ds(2, 1), w_s, :])
    d_s.add("f", 24, wps.at[pl.ds(2, 1), pl.ds(0, HW), :], wx.at[pl.ds(2, 1), w_n, :])

    def start(c):
        c.start()

    def wait_send(c):
        c.wait_send()

    def wait_recv(c):
        c.wait_recv()

    g_n.each(["k"], start)
    g_s.each(["k"], start)

    def load_done(f, src):
        pltpu.make_async_copy(src, xb.at[f, :, pl.ds(PAD, NB), :], lsem.at[f]).wait()
        g_n.each([("x", f)], start)
        g_s.each([("x", f)], start)

    def pack_tile(t):
        items = pack_items(t)

        def body(c, carry):
            r = pl.multiple_of(c * R, R)
            rows = pl.ds(pl.multiple_of(c * R + PAD, PAD), R)
            half = lanes(R) // 2
            acc = jnp.zeros((R, NB), f32)
            for f, k, off in items:
                acc = jnp.where(half == off // 2, roll(xb[f, k, rows, :], (off + 1) % NB), acc)
            if t == 2:
                for i, lane in ((0, L_KMT), (1, L_DEP)):
                    off = lane % NB
                    acc = jnp.where(half == off // 2, roll(kd[i, rows, :], (off + 1) % NB), acc)
            pks[t, pl.ds(r, R), :] = acc
            return carry
        lax.fori_loop(0, CH, body, 0)
        g_c.each([("p", t)], start)

    load_done(0, u_h)
    load_done(1, v_h)
    pack_tile(0)
    load_done(2, t_h)
    load_done(3, s_h)
    pack_tile(1)
    pack_tile(2)
    d_n.each(["p"], start)
    d_s.each(["p"], start)
    for g in (g_c, g_n, g_s, d_n, d_s):
        g.each(["w"], start)

    def pressure(r, rows_n):
        rows = pl.ds(r, rows_n)
        km = kd[0, rows, :]
        th = kd[1, rows, :] / jnp.maximum(km, 1.0)

        def level(k, cum):
            rho = jnp.where(k.astype(f32) < km, BETA_S * xb[3, k, rows, :] - ALPHA_T * xb[2, k, rows, :], 0.0)
            new = cum + rho
            pb[k, rows, :] = (new - 0.5 * rho) * th
            return new
        lax.fori_loop(0, LV, level, jnp.zeros((rows_n, NB), f32))

    for c in range(CH):
        pressure(PAD + c * R, R)

    near = [("x", f) for f in range(4)] + ["k"]
    Group_s = Group(has_s, None)
    Group_s.copies = {**g_n.copies, **{("d", k): c for k, c in d_n.copies.items()}}
    Group_n = Group(has_n, None)
    Group_n.copies = {**g_s.copies, **{("d", k): c for k, c in d_s.copies.items()}}
    Group_s.each(near + [("d", "p")], wait_recv)
    Group_n.each(near + [("d", "p")], wait_recv)
    g_c.each([("p", t) for t in range(3)], wait_recv)

    pressure(PAD + NB, PAD)
    mid = pl.ds(PAD, NB)
    pz[0] = pk[0, mid, :] + pk[0, pl.ds(PAD + 1, NB), :]
    pw[0] = pk[0, mid, :] + pk[0, pl.ds(PAD - 1, NB), :]
    pw[1] = pk[1, mid, :] + pk[1, pl.ds(PAD - 1, NB), :]

    def momentum(c):
        r = PAD + c * R
        rows, rows_n, rows_s = pl.ds(r, R), pl.ds(r + 1, R), pl.ds(r - 1, R)
        q = pl.ds(c * R, R)
        lane = lanes(R)
        l0, l127 = lane == 0, lane == NB - 1
        km = kd[0, rows, :]
        dm = kd[1, rows, :]
        hk = halo_lanes(pk, L_KMT, rows)
        hd = halo_lanes(pk, L_DEP, rows)
        hth = hd / jnp.maximum(hk, 1.0)
        nu = jnp.minimum(km, east(km, hk, l0))
        nv = jnp.minimum(km, kd[0, rows_n, :])

        def level(k, carry):
            hc, gus, gvs, du, dv = carry
            kf = k.astype(f32)
            u, un, us = xb[0, k, rows, :], xb[0, k, rows_n, :], xb[0, k, rows_s, :]
            v, vn, vs = xb[1, k, rows, :], xb[1, k, rows_n, :], xb[1, k, rows_s, :]
            hu = halo_lanes(pk, 2 * k, rows)
            hv = halo_lanes(pk, F_STRIDE + 2 * k, rows)
            ht = halo_lanes(pk, 2 * F_STRIDE + 2 * k, rows)
            hs_ = halo_lanes(pk, 3 * F_STRIDE + 2 * k, rows)
            hz = halo_lanes(pz, 2 * k, q)
            hw = halo_lanes(pw, F_STRIDE + 2 * k, q)
            ue, uw = east(u, hu, l0), west(u, hu, l127)
            ve, vw = east(v, hv, l0), west(v, hv, l127)
            w = v + vs
            z = u + un
            w4 = 0.25 * (w + east(w, hw, l0))
            z4 = 0.25 * (z + west(z, hz, l127))
            p, pn = pb[k, rows, :], pb[k, rows_n, :]
            hrho = jnp.where(kf < hk, BETA_S * hs_ - ALPHA_T * ht, 0.0)
            hc = hc + hrho
            pe = east(p, (hc - 0.5 * hrho) * hth, l0)
            gu = p - pe - 0.5 * (u * (ue - uw) + w4 * (un - us))
            gv = p - pn - 0.5 * (z4 * (ve - vw) + v * (vn - vs))
            mu, mv = kf < nu, kf < nv
            gu = jnp.where(mu, gu, 0.0)
            gv = jnp.where(mv, gv, 0.0)
            inner, last = tab[0, k], tab[1, k]
            fu = jnp.where(kf < nu - 1.0, inner, jnp.where(mu, last, 0.0))
            fv = jnp.where(kf < nv - 1.0, inner, jnp.where(mv, last, 0.0))
            du = fu * (u + ADV_COURANT * gu + VISC_NUM * du)
            dv = fv * (v + ADV_COURANT * gv + VISC_NUM * dv)
            u2[k, q, :] = du
            v2[k, q, :] = dv
            return hc, gus + gu, gvs + gv, du, dv

        zero = jnp.zeros((R, NB), f32)
        _, gus, gvs, _, _ = lax.fori_loop(0, LV, level, (zero,) * 5)
        de = east(dm, hd, l0)
        dn = kd[1, rows_n, :]
        hu_ = jnp.where(nu > 0, 0.5 * (dm + de), 0.0)
        hv_ = jnp.where(nv > 0, 0.5 * (dm + dn), 0.0)
        fx = hu_ * gus / jnp.maximum(nu, 1.0)
        fy = hv_ * gvs / jnp.maximum(nv, 1.0)
        wo[4, pl.ds(HW + c * R, R), :] = fx
        wo[5, pl.ds(HW + c * R, R), :] = fy
        wps[2, q, :] = pair(fx, fy)

    for c in range(CH):
        momentum(c)
    for g in (g_c, g_n, g_s, d_n, d_s):
        g.each(["f"], start)

    def back(c):
        r = PAD + c * R
        rows, q = pl.ds(r, R), pl.ds(c * R, R)
        lane = lanes(R)
        km = kd[0, rows, :]
        hk = halo_lanes(pk, L_KMT, rows)
        nu = jnp.minimum(km, east(km, hk, lane == 0))
        nv = jnp.minimum(km, kd[0, pl.ds(r + 1, R), :])

        def level(i, carry):
            xu, xv, su, sv = carry
            k = LV - 1 - i
            ratio = tab[2, k]
            xu = u2[k, q, :] + ratio * xu
            xv = v2[k, q, :] + ratio * xv
            u2[k, q, :] = xu
            v2[k, q, :] = xv
            return xu, xv, su + xu, sv + xv

        zero = jnp.zeros((R, NB), f32)
        _, _, su, sv = lax.fori_loop(0, LV, level, (zero,) * 4)
        mean[0, q, :] = su / jnp.maximum(nu, 1.0)
        mean[1, q, :] = sv / jnp.maximum(nv, 1.0)

    for c in range(CH):
        back(c)

    def halo_rows(k, carry):
        for f in range(4):
            rowh[f, pl.ds(k, 1), :] = xb[f, k, hs, :]
            rowh[4 + f, pl.ds(k, 1), :] = xb[f, k, hn, :]
        return carry
    lax.fori_loop(0, LV, halo_rows, 0)
    pko[...] = pk[:, mid, :]
    kdo[...] = kd[0]

    g_c.each(["w", "f"], wait_recv)
    Group_s.each(["w", "f", ("d", "w"), ("d", "f")], wait_recv)
    Group_n.each(["w", "f", ("d", "w"), ("d", "f")], wait_recv)

    ETA, U, V, WU, WV, PU, PV, WC = range(8)
    for i in range(8):
        for t in range(2):
            for r in (0, PAD + NW):
                bt[i, t, pl.ds(r, PAD), :] = jnp.zeros((PAD, NB), f32)

    def unpack(c, carry):
        src = pl.ds(pl.multiple_of(c * R, R), R)
        dst = pl.ds(pl.multiple_of(c * R + PAD, PAD), R)
        e1, u1 = unpair(wx[0, src, :])
        v1, d1 = unpair(wx[1, src, :])
        x1, y1 = unpair(wx[2, src, :])
        for t, (e, u, v, d, x, y) in enumerate((tuple(wo[i, src, :] for i in range(6)), (e1, u1, v1, d1, x1, y1))):
            bt[ETA, t, dst, :] = e
            bt[U, t, dst, :] = u
            bt[V, t, dst, :] = v
            bt[WC, t, dst, :] = d
            bt[PU, t, dst, :] = (ADV_COURANT / SUBCYCLES) * x
            bt[PV, t, dst, :] = (ADV_COURANT / SUBCYCLES) * y
        return carry
    lax.fori_loop(0, NW // R, unpack, 0)

    wchunks = [PAD + c * R for c in range(NW // R)]
    l0, l127 = lanes(R) == 0, lanes(R) == NB - 1
    for r in wchunks:
        rows = pl.ds(r, R)
        d = [bt[WC, t, rows, :] for t in range(2)]
        dn = [bt[WC, t, pl.ds(r + 1, R), :] for t in range(2)]
        for t in range(2):
            de = east(d[t], d[1 - t], l0)
            fu = (d[t] > 0) & (de > 0)
            fv = (d[t] > 0) & (dn[t] > 0)
            bt[WU, t, rows, :] = jnp.where(fu, WAVE_COURANT * (0.5 * (d[t] + de)), 0.0)
            bt[WV, t, rows, :] = jnp.where(fv, WAVE_COURANT * (0.5 * (d[t] + dn[t])), 0.0)
            bt[U, t, rows, :] = jnp.where(fu, bt[U, t, rows, :], 0.0)
            bt[V, t, rows, :] = jnp.where(fv, bt[V, t, rows, :], 0.0)
            bt[ETA, t, rows, :] = jnp.where(d[t] > 0, bt[ETA, t, rows, :], 0.0)
    for r in wchunks:
        for t in range(2):
            bt[WC, t, pl.ds(r, R), :] = jnp.where(bt[WC, t, pl.ds(r, R), :] > 0, WAVE_COURANT, 0.0)
    corr[...] = jnp.zeros((2, NB, NB), f32)

    def subcycle(n, carry):
        wn = tab[6, n]
        for r in wchunks:
            rows = pl.ds(r, R)
            uu = [bt[U, t, rows, :] for t in range(2)]
            for t in range(2):
                uw = west(uu[t], uu[1 - t], l127)
                div = uu[t] - uw + bt[V, t, rows, :] - bt[V, t, pl.ds(r - 1, R), :]
                bt[ETA, t, rows, :] = bt[ETA, t, rows, :] - bt[WC, t, rows, :] * div
        for i, r in enumerate(wchunks):
            rows = pl.ds(r, R)
            ee = [bt[ETA, t, rows, :] for t in range(2)]
            for t in range(2):
                xe = east(ee[t], ee[1 - t], l0)
                xn = bt[ETA, t, pl.ds(r + 1, R), :]
                un = bt[U, t, rows, :] - bt[WU, t, rows, :] * (xe - ee[t]) + bt[PU, t, rows, :]
                vn = bt[V, t, rows, :] - bt[WV, t, rows, :] * (xn - ee[t]) + bt[PV, t, rows, :]
                bt[U, t, rows, :] = un
                bt[V, t, rows, :] = vn
                if t == 0 and HW + PAD <= r < HW + PAD + NB:
                    q = pl.ds(r - HW - PAD, R)
                    corr[0, q, :] = corr[0, q, :] + wn * un
                    corr[1, q, :] = corr[1, q, :] + wn * vn
        return carry
    lax.fori_loop(0, SUBCYCLES, subcycle, 0)

    core = pl.ds(PAD + HW, NB)
    eta_o[...] = bt[ETA, 0, core, :]
    tu_o[...] = bt[U, 0, core, :]
    tv_o[...] = bt[V, 0, core, :]
    for i, w in ((0, WU), (1, WV)):
        depth = bt[w, 0, core, :] * (1.0 / WAVE_COURANT)
        corr[i] = corr[i] / jnp.where(depth > 0, depth, 1.0) - mean[i]

    g_c.each(list(g_c.copies), wait_send)
    for g in (g_n, g_s, d_n, d_s):
        g.each(list(g.copies), wait_send)


def tracer_kernel(tab, u_h, v_h, t_h, s_h, rowh, pk, kd, u2, v2, corr, eta_r, tu_r, tv_r,
                  eta_o, tu_o, tv_o, uo_h, vo_h, to_h, so_h,
                  xb, out, lsem, osem):
    srcs = (u_h, v_h, t_h, s_h)
    outs = (uo_h, vo_h, to_h, so_h)

    def load(f, c):
        return pltpu.make_async_copy(srcs[f].at[:, pl.ds(c * R, R), :], xb.at[f, :, pl.ds(PAD + c * R, R), :], lsem.at[f, c])

    def store(f, c):
        return pltpu.make_async_copy(out.at[f, :, pl.ds(c * R, R), :], outs[f].at[:, pl.ds(c * R, R), :], osem.at[f, c])

    for c in range(CH):
        for f in range(4):
            load(f, c).start()

    eta_o[...] = eta_r[...]
    tu_o[...] = tu_r[...]
    tv_o[...] = tv_r[...]

    def halo_rows(k, carry):
        for f in range(1, 4):
            xb[f, k, pl.ds(PAD - 1, 1), :] = rowh[f, pl.ds(k, 1), :]
            xb[f, k, pl.ds(PAD + NB, 1), :] = rowh[4 + f, pl.ds(k, 1), :]
        return carry
    lax.fori_loop(0, LV, halo_rows, 0)

    def chunk(c):
        r = PAD + c * R
        rows, rows_n, rows_s = pl.ds(r, R), pl.ds(r + 1, R), pl.ds(r - 1, R)
        q = pl.ds(c * R, R)
        lane = lanes(R)
        l0, l127 = lane == 0, lane == NB - 1
        km = kd[rows, :]
        hk = halo_lanes(pk, L_KMT, q)
        nu = jnp.minimum(km, east(km, hk, l0))
        nuw = jnp.minimum(km, west(km, hk, l127))
        nv = jnp.minimum(km, kd[rows_n, :])
        nvs = jnp.minimum(km, kd[rows_s, :])

        def level(k, carry):
            kf = k.astype(f32)
            u, v, vs = xb[0, k, rows, :], xb[1, k, rows, :], xb[1, k, rows_s, :]
            uw = west(u, halo_lanes(pk, 2 * k, q), l127)
            u = jnp.where(kf < nu, ADV_COURANT * u, 0.0)
            uw = jnp.where(kf < nuw, ADV_COURANT * uw, 0.0)
            v = jnp.where(kf < nv, ADV_COURANT * v, 0.0)
            vs = jnp.where(kf < nvs, ADV_COURANT * vs, 0.0)
            um, vm = jnp.minimum(u, 0.0), jnp.minimum(v, 0.0)
            uwp, vsp = jnp.maximum(uw, 0.0), jnp.maximum(vs, 0.0)
            here = 1.0 - ((u - um) - (uw - uwp) + (v - vm) - (vs - vsp))
            f = jnp.where(kf < km - 1.0, tab[3, k], jnp.where(kf < km, tab[4, k], 0.0))
            new = []
            for i in (2, 3):
                t = xb[i, k, rows, :]
                h = halo_lanes(pk, i * F_STRIDE + 2 * k, q)
                adv = here * t - um * east(t, h, l0) + uwp * west(t, h, l127) - vm * xb[i, k, rows_n, :] + vsp * xb[i, k, rows_s, :]
                d = f * (adv + DIFF_NUM * carry[i - 2])
                out[i, k, q, :] = d
                new.append(d)
            return tuple(new)

        zero = jnp.zeros((R, NB), f32)
        lax.fori_loop(0, LV, level, (zero, zero))
        cu, cv = corr[0, q, :], corr[1, q, :]

        def back(i, carry):
            xt, xs = carry
            k = LV - 1 - i
            kf = k.astype(f32)
            ratio = tab[5, k]
            xt = out[2, k, q, :] + ratio * xt
            xs = out[3, k, q, :] + ratio * xs
            out[2, k, q, :] = xt
            out[3, k, q, :] = xs
            out[0, k, q, :] = u2[k, q, :] + jnp.where(kf < nu, cu, 0.0)
            out[1, k, q, :] = v2[k, q, :] + jnp.where(kf < nv, cv, 0.0)
            return xt, xs
        lax.fori_loop(0, LV, back, (zero, zero))

    for f in range(4):
        load(f, 0).wait()
    for c in range(CH):
        if c + 1 < CH:
            for f in range(4):
                load(f, c + 1).wait()
        chunk(c)
        for f in range(4):
            store(f, c).start()
    for c in range(CH):
        for f in range(4):
            store(f, c).wait()


def solution(mesh):
    nrow = mesh.shape["row"]
    vm = pl.BlockSpec(memory_space=pltpu.VMEM)
    sm = pl.BlockSpec(memory_space=pltpu.SMEM)
    hb = pl.BlockSpec(memory_space=pltpu.HBM)
    table = solver_tables()

    def sds(*shape):
        return jax.ShapeDtypeStruct(shape, f32)

    def step(u, v, t, s, eta, tu, tv, depth, kmt):
        tab = jnp.asarray(table)
        rowh, pk, kd, u2, v2, corr, eta1, tu1, tv1 = pl.pallas_call(
            functools.partial(momentum_kernel, nrow),
            out_shape=(sds(8, LV, NB), sds(3, NB, NB), sds(NP, NB), sds(LV, NB, NB), sds(LV, NB, NB),
                       sds(2, NB, NB), sds(NB, NB), sds(NB, NB), sds(NB, NB)),
            in_specs=[sm] + [hb] * 4 + [vm] * 5,
            out_specs=(vm,) * 9,
            scratch_shapes=[
                pltpu.VMEM((4, LV, NP, NB), f32),
                pltpu.VMEM((LV, NP, NB), f32),
                pltpu.VMEM((3, NP, NB), f32),
                pltpu.VMEM((3, NB, NB), f32),
                pltpu.VMEM((1, NB, NB), f32),
                pltpu.VMEM((2, NB, NB), f32),
                pltpu.VMEM((2, NP, NB), f32),
                pltpu.VMEM((6, NW, NB), f32),
                pltpu.VMEM((3, NW, NB), f32),
                pltpu.VMEM((3, NB, NB), f32),
                pltpu.VMEM((8, 2, NWP, NB), f32),
                pltpu.VMEM((2, NB, NB), f32),
                pltpu.SemaphoreType.DMA((4,)),
                pltpu.SemaphoreType.DMA((25,)),
                pltpu.SemaphoreType.DMA((25,)),
            ],
            compiler_params=pltpu.CompilerParams(collective_id=0, has_side_effects=True, vmem_limit_bytes=34 * 2 ** 20),
            name="momentum",
        )(tab, u, v, t, s, eta, tu, tv, depth, kmt)
        return pl.pallas_call(
            tracer_kernel,
            out_shape=(sds(NB, NB),) * 3 + (sds(LV, NB, NB),) * 4,
            in_specs=[sm] + [hb] * 4 + [vm] * 9,
            out_specs=(vm,) * 3 + (hb,) * 4,
            scratch_shapes=[
                pltpu.VMEM((4, LV, NP, NB), f32),
                pltpu.VMEM((4, LV, NB, NB), f32),
                pltpu.SemaphoreType.DMA((4, CH)),
                pltpu.SemaphoreType.DMA((4, CH)),
            ],
            compiler_params=pltpu.CompilerParams(vmem_limit_bytes=34 * 2 ** 20),
            name="tracers",
        )(tab, u, v, t, s, rowh, pk, kd, u2, v2, corr, eta1, tu1, tv1)

    s3, s2 = P(None, "row", "col"), P("row", "col")
    return jax.shard_map(step, mesh=mesh, in_specs=(s3,) * 4 + (s2,) * 5,
                         out_specs=(s2,) * 3 + (s3,) * 4, check_vma=False)
```

time: 1180 us -> 107 us (0.09)
  the two profiles are of different devices: /device:TPU:12 before, /device:TPU:0 now
where the time goes in v1:
time: 107 us; the launch traced here: 106 us
  Pallas kernels  93.9 us (88%)
  local copies, waits for them, and re-layouts  11.9 us (11%)
    pallas_call x1, Pallas kernels, step(): pl.pallas_call(functools.partial(momentum_kernel, nrow), out_shape=(sds(8...  59 us
    pallas_call x1, Pallas kernels, step(): pl.pallas_call(tracer_kernel, out_shape=(sds(NB, NB),) * 3 + (sds(LV, NB,...  34.9 us
    unnamed x20, local copies, waits for them, and re-layouts  11.9 us

profile of v1, /device:TPU:0, one launch (start us, length us, event | category | flops | bytes accessed | tf_op | source)
XLA Modules:
  0.0 106.4 jit_solution(9440233528624270792)
XLA Ops:
  0.6 0.0 copy-start
  0.6 1.7 %copy-done = f32[41,128,128]{2,1,0:T(8,128)S(1)} copy-done((f32[41,128,128]{2,1,0:T(8,128)S(1)}, f32[41,128,128]{2,1,0:T(8,128)}, u32[]{:S(2)}) %copy-start) | copy-done | bytes 2687000
  2.4 0.0 copy-start.1
  2.4 1.8 %copy-done.1 = f32[41,128,128]{2,1,0:T(8,128)S(1)} copy-done((f32[41,128,128]{2,1,0:T(8,128)S(1)}, f32[41,128,128]{2,1,0:T(8,128)}, u32[]{:S(2)}) %copy-start.1) | copy-done | bytes 2687000
  4.2 0.0 copy-start.2
  4.2 1.8 %copy-done.2 = f32[41,128,128]{2,1,0:T(8,128)S(1)} copy-done((f32[41,128,128]{2,1,0:T(8,128)S(1)}, f32[41,128,128]{2,1,0:T(8,128)}, u32[]{:S(2)}) %copy-start.2) | copy-done | bytes 2687000
  5.9 0.0 copy-start.3
  5.9 1.8 %copy-done.3 = f32[41,128,128]{2,1,0:T(8,128)S(1)} copy-done((f32[41,128,128]{2,1,0:T(8,128)S(1)}, f32[41,128,128]{2,1,0:T(8,128)}, u32[]{:S(2)}) %copy-start.3) | copy-done | bytes 2687000
  7.7 0.0 copy-start.4
  7.7 0.8 copy-done.4
  8.5 0.0 copy-start.5
  8.5 0.8 copy-done.5
  9.4 0.0 copy-start.6
  9.4 0.8 copy-done.6
  10.2 0.0 copy-start.7
  10.2 0.8 copy-done.7
  11.0 0.0 copy-start.8
  11.0 0.8 copy-done.8
  11.9 0.0 copy-start.9
  11.9 0.7 copy-done.9
  12.6 59.0 %momentum.1 = (f32[8,41,128]{2,1,0:T(8,128)S(1)}, f32[3,128,128]{2,1,0:T(8,128)S(1)}, f32[144,128]{1,0:T(8,128)S(1)}, f32[41,128,128]{2,1,0:T(8,128)S(1)}, f32[4...) custom-call(f32[8,128]{1,0:T(8,128)S(1)} %copy-done.9, ...), custom_call_target="tpu_custom_call" | custom-call | tf_op jit(solution)/shard_map/momentum/pallas_call | solution.py:573
  71.6 34.9 %tracers.1 = (f32[128,128]{1,0:T(8,128)}, f32[128,128]{1,0:T(8,128)}, f32[128,128]{1,0:T(8,128)}, f32[41,128,128]{2,1,0:T(8,128)}, f32[41,128,128]{2,1,0:T(8,128...) custom-call(f32[8,128]{1,0:T(8,128)S(1)} %copy-done.9, f32[41,128,128]{2,1,0:T(8,128)S(1)} %copy-done, ...), custom_call_target="tpu_custom_call" | custom-call | tf_op jit(solution)/shard_map/tracers/pallas_call | solution.py:599
Async XLA Ops:
  0.6 1.8 %copy-start = (f32[41,128,128]{2,1,0:T(8,128)S(1)}, f32[41,128,128]{2,1,0:T(8,128)}, u32[]{:S(2)}) copy-start(f32[41,128,128]{2,1,0:T(8,128)} %u_h.3) | copy-start | bytes 8060932
  2.4 1.8 %copy-start.1 = (f32[41,128,128]{2,1,0:T(8,128)S(1)}, f32[41,128,128]{2,1,0:T(8,128)}, u32[]{:S(2)}) copy-start(f32[41,128,128]{2,1,0:T(8,128)} %v_h.3) | copy-start | bytes 8060932
  4.2 1.8 %copy-start.2 = (f32[41,128,128]{2,1,0:T(8,128)S(1)}, f32[41,128,128]{2,1,0:T(8,128)}, u32[]{:S(2)}) copy-start(f32[41,128,128]{2,1,0:T(8,128)} %t_h.3) | copy-start | bytes 8060932
  5.9 1.8 %copy-start.3 = (f32[41,128,128]{2,1,0:T(8,128)S(1)}, f32[41,128,128]{2,1,0:T(8,128)}, u32[]{:S(2)}) copy-start(f32[41,128,128]{2,1,0:T(8,128)} %s_h.3) | copy-start | bytes 8060932
  7.7 0.8 copy-start.4
  8.5 0.8 copy-start.5
  9.4 0.8 copy-start.6
  10.2 0.8 copy-start.7
  11.0 0.8 copy-start.8
  11.9 0.7 copy-start.9

commit v2 on v1

v2 whole, which is shorter than its diff:
```python
import functools

import jax
import jax.numpy as jnp
import numpy as np
from jax import lax
from jax.experimental import pallas as pl
from jax.experimental.pallas import tpu as pltpu
from jax.sharding import PartitionSpec as P

SUBCYCLES = 30
ADV_COURANT = 0.25
WAVE_COURANT = 0.5
VISC_NUM = 4.0
DIFF_NUM = 1.0
ALPHA_T = 0.3
BETA_S = 0.6

MESH = pl.DeviceIdType.MESH
f32 = jnp.float32

LV = 41
NB = 128
PAD = 8
NP = NB + 2 * PAD
HW = 32
NW = NB + 2 * HW
NWP = NW + 2 * PAD
R = 32
CH = NB // R
L_EXTRA = 2 * LV


def solver_tables():
    out = np.zeros((8, 128), np.float64)
    for base, a in ((0, VISC_NUM), (3, DIFF_NUM)):
        c = 0.0
        for k in range(LV):
            lo = a if k > 0 else 0.0
            inner = 1.0 / (1.0 + a + lo - lo * c)
            last = 1.0 / (1.0 + lo - lo * c)
            out[base, k] = inner
            out[base + 1, k] = last
            c = a * inner
            out[base + 2, k] = c
    s = np.arange(1, SUBCYCLES + 1) / (SUBCYCLES + 1)
    w = s ** 2 * (1.0 - s ** 4)
    out[6, :SUBCYCLES] = w / w.sum()
    return out.astype(np.float32)


def lanes(rows):
    return lax.broadcasted_iota(jnp.int32, (rows, NB), 1)


def roll(x, s):
    return pltpu.roll(x, s, 1)


def east(x, halo, l0):
    return roll(jnp.where(l0, halo, x), NB - 1)


def west(x, halo, l127):
    return roll(jnp.where(l127, halo, x), 1)


def levels(body, init, step):
    def trip(i, carry):
        for j in range(step):
            carry = body(i * step + j, carry)
        return carry
    carry = lax.fori_loop(0, LV // step, trip, init)
    for k in range(LV // step * step, LV):
        carry = body(jnp.int32(k), carry)
    return carry


def pair(a, b):
    return jnp.where(lanes(a.shape[0]) < 64, roll(a, 32), roll(b, 96))


def unpair(p):
    l = lanes(p.shape[0])
    ok = (l < HW) | (l >= NB - HW)
    return jnp.where(ok, roll(p, 96), 0.0), jnp.where(ok, roll(p, 32), 0.0)


def main_kernel(nrow, tab, u_h, v_h, t_h, s_h, eta_r, tu_r, tv_r, dep_r, kmt_r,
                u2, v2, t2, s2, corr, faces, eta_o, tu_o, tv_o,
                xb, sp, sh, pb, cum, hb, pk, pks, pzw, kd, wo, wx, wps, bt, mean,
                lsem, ssem, rsem):
    col = lax.axis_index("col")
    row = lax.axis_index("row")
    oc = 1 - col
    has_n = row < nrow - 1
    has_s = row > 0

    for f, src in enumerate((u_h, v_h, t_h, s_h)):
        pltpu.make_async_copy(src, xb.at[f, :, pl.ds(PAD, NB), :], lsem.at[f]).start()

    def at_wall(edge, rows, wrows):
        @pl.when(edge)
        def _():
            kd[:, rows, :] = jnp.zeros((2, PAD, NB), f32)
            pk[:, rows, :] = jnp.zeros((4, PAD, NB), f32)
            wo[:, wrows, :] = jnp.zeros((6, HW, NB), f32)
            wx[:, wrows, :] = jnp.zeros((3, HW, NB), f32)

            def zero(k, c):
                for f in range(4):
                    xb[f, k, rows, :] = jnp.zeros((PAD, NB), f32)
                return c
            lax.fori_loop(0, LV, zero, 0)

    at_wall(jnp.logical_not(has_s), pl.ds(0, PAD), pl.ds(0, HW))
    at_wall(jnp.logical_not(has_n), pl.ds(PAD + NB, PAD), pl.ds(HW + NB, HW))

    bar = pltpu.get_barrier_semaphore()

    def greet(dev):
        pl.semaphore_signal(bar, inc=1, device_id=dev, device_id_type=MESH)

    greet({"col": oc, "row": row})

    @pl.when(has_n)
    def _():
        greet({"col": col, "row": row + 1})
        greet({"col": oc, "row": row + 1})

    @pl.when(has_s)
    def _():
        greet({"col": col, "row": row - 1})
        greet({"col": oc, "row": row - 1})

    kmf = kmt_r[...].astype(f32)
    dm = jnp.where(kmt_r[...] > 0, dep_r[...], 0.0)
    kd[0, pl.ds(PAD, NB), :] = kmf
    kd[1, pl.ds(PAD, NB), :] = dm
    own = pl.ds(HW, NB)
    wo[0, own, :] = eta_r[...]
    wo[1, own, :] = tu_r[...]
    wo[2, own, :] = tv_r[...]
    wo[3, own, :] = dm
    wps[0] = pair(eta_r[...], tu_r[...])
    wps[1] = pair(tv_r[...], dm)

    pl.semaphore_wait(bar, 1 + 2 * has_n.astype(jnp.int32) + 2 * has_s.astype(jnp.int32))

    class Group:
        def __init__(self, cond, dev):
            self.cond, self.dev, self.copies = cond, dev, {}

        def add(self, key, sem, src, dst):
            self.copies[key] = pltpu.make_async_remote_copy(
                src_ref=src, dst_ref=dst, send_sem=ssem.at[sem], recv_sem=rsem.at[sem],
                device_id=self.dev, device_id_type=MESH)

        def each(self, keys, what):
            def run():
                for key in keys:
                    what(self.copies[key])
            if self.cond is None:
                run()
            else:
                pl.when(self.cond)(run)

    g_c = Group(None, {"col": oc, "row": row})
    g_n = Group(has_n, {"col": col, "row": row + 1})
    g_s = Group(has_s, {"col": col, "row": row - 1})
    d_n = Group(has_n, {"col": oc, "row": row + 1})
    d_s = Group(has_s, {"col": oc, "row": row - 1})
    hi, lo = pl.ds(PAD + NB - 1, 1), pl.ds(PAD, 1)
    hs, hn = pl.ds(PAD - 1, 1), pl.ds(PAD + NB, 1)
    w_hi, w_lo = pl.ds(NB, HW), pl.ds(HW, HW)
    w_s, w_n = pl.ds(0, HW), pl.ds(HW + NB, HW)
    for t in range(4):
        g_c.add(("p", t), 25 + t, pks.at[t], pk.at[t, pl.ds(PAD, NB), :])
    g_c.add("w", 3, wps.at[pl.ds(0, 2)], wx.at[pl.ds(0, 2), own, :])
    g_c.add("f", 4, wps.at[pl.ds(2, 1)], wx.at[pl.ds(2, 1), own, :])
    for f in range(4):
        g_n.add(("x", f), 5 + f, xb.at[f, :, hi, :], xb.at[f, :, hs, :])
        g_s.add(("x", f), 9 + f, xb.at[f, :, lo, :], xb.at[f, :, hn, :])
    g_n.add("k", 13, kd.at[:, hi, :], kd.at[:, hs, :])
    g_s.add("k", 14, kd.at[:, lo, :], kd.at[:, hn, :])
    g_n.add("w", 15, wo.at[pl.ds(0, 4), w_hi, :], wo.at[pl.ds(0, 4), w_s, :])
    g_s.add("w", 16, wo.at[pl.ds(0, 4), w_lo, :], wo.at[pl.ds(0, 4), w_n, :])
    g_n.add("f", 17, wo.at[pl.ds(4, 2), w_hi, :], wo.at[pl.ds(4, 2), w_s, :])
    g_s.add("f", 18, wo.at[pl.ds(4, 2), w_lo, :], wo.at[pl.ds(4, 2), w_n, :])
    d_n.add("p", 19, pks.at[pl.ds(0, 2), pl.ds(NB - 1, 1), :], pk.at[pl.ds(0, 2), hs, :])
    d_s.add("p", 20, pks.at[pl.ds(0, 2), pl.ds(0, 1), :], pk.at[pl.ds(0, 2), hn, :])
    d_n.add("w", 21, wps.at[pl.ds(0, 2), pl.ds(NB - HW, HW), :], wx.at[pl.ds(0, 2), w_s, :])
    d_s.add("w", 22, wps.at[pl.ds(0, 2), pl.ds(0, HW), :], wx.at[pl.ds(0, 2), w_n, :])
    d_n.add("f", 23, wps.at[pl.ds(2, 1), pl.ds(NB - HW, HW), :], wx.at[pl.ds(2, 1), w_s, :])
    d_s.add("f", 24, wps.at[pl.ds(2, 1), pl.ds(0, HW), :], wx.at[pl.ds(2, 1), w_n, :])

    def start(c):
        c.start()

    def wait_send(c):
        c.wait_send()

    def wait_recv(c):
        c.wait_recv()

    g_n.each(["k"], start)
    g_s.each(["k"], start)

    def load_and_pack(f, src):
        pltpu.make_async_copy(src, xb.at[f, :, pl.ds(PAD, NB), :], lsem.at[f]).wait()
        g_n.each([("x", f)], start)
        g_s.each([("x", f)], start)

        def body(c, carry):
            rows = pl.ds(pl.multiple_of(c * R + PAD, PAD), R)
            half = lanes(R) // 2
            acc = jnp.zeros((R, NB), f32)
            for k in range(LV):
                acc = jnp.where(half == k, roll(xb[f, k, rows, :], 2 * k + 1), acc)
            if f < 2:
                acc = jnp.where(half == LV, roll(kd[f, rows, :], L_EXTRA + 1), acc)
            pks[f, pl.ds(pl.multiple_of(c * R, R), R), :] = acc
            return carry
        lax.fori_loop(0, CH, body, 0)
        g_c.each([("p", f)], start)

    load_and_pack(0, u_h)
    load_and_pack(1, v_h)
    d_n.each(["p"], start)
    d_s.each(["p"], start)
    load_and_pack(2, t_h)
    load_and_pack(3, s_h)
    for g in (g_c, g_n, g_s, d_n, d_s):
        g.each(["w"], start)

    mid = pl.ds(PAD, NB)
    cum[...] = jnp.zeros((NB, NB), f32)

    def shift_trip(ks):
        for f in range(4):
            for k in ks:
                for c in range(CH):
                    rows = pl.ds(PAD + c * R, R)
                    x = xb[f, k, rows, :]
                    q = pl.ds(c * R, R)
                    xe, xw = roll(x, NB - 1), roll(x, 1)
                    if f == 0:
                        sh[0, k, q, :] = xe
                        sp[0, k, rows, :] = xw
                    elif f == 1:
                        sp[1, k, rows, :] = xe
                        sh[1, k, q, :] = xw
                    else:
                        sh[2 * f - 2, k, q, :] = xe
                        sh[2 * f - 1, k, q, :] = xw
        for c in range(CH):
            rows, q = pl.ds(PAD + c * R, R), pl.ds(c * R, R)
            depth_of(rows, q, ks)

    def depth_of(rows, q, ks):
        km = kd[0, rows, :]
        th = kd[1, rows, :] / jnp.maximum(km, 1.0)
        total = cum[q, :]
        for k in ks:
            rho = jnp.where(jnp.asarray(k, f32) < km, BETA_S * xb[3, k, rows, :] - ALPHA_T * xb[2, k, rows, :], 0.0)
            new = total + rho
            pb[k, rows, :] = (new - 0.5 * rho) * th
            total = new
        cum[q, :] = total

    def shift_body(i, carry):
        shift_trip([4 * i + j for j in range(4)])
        return carry
    lax.fori_loop(0, LV // 4, shift_body, 0)
    shift_trip([LV - 1])

    near = [("x", f) for f in range(4)] + ["k"]
    from_s = Group(has_s, None)
    from_s.copies = {**g_n.copies, **{("d", k): c for k, c in d_n.copies.items()}}
    from_n = Group(has_n, None)
    from_n.copies = {**g_s.copies, **{("d", k): c for k, c in d_s.copies.items()}}
    from_s.each(near + [("d", "p")], wait_recv)
    from_n.each(near + [("d", "p")], wait_recv)

    below, above = pl.ds(0, PAD), pl.ds(PAD + NB, PAD)
    for k in range(LV):
        sp[0, k, above, :] = roll(xb[0, k, above, :], 1)
        sp[1, k, below, :] = roll(xb[1, k, below, :], NB - 1)
    cum[pl.ds(0, PAD), :] = jnp.zeros((PAD, NB), f32)
    depth_of(above, pl.ds(0, PAD), list(range(LV)))

    g_c.each([("p", t) for t in range(4)], wait_recv)
    odd = lanes(NB) % 2 == 1
    pzw[...] = jnp.where(odd, pk[1, mid, :] + pk[1, pl.ds(PAD - 1, NB), :], pk[0, mid, :] + pk[0, pl.ds(PAD + 1, NB), :])

    def columns(c):
        r = PAD + c * R
        rows, rows_n, rows_s = pl.ds(r, R), pl.ds(r + 1, R), pl.ds(r - 1, R)
        q = pl.ds(c * R, R)
        lane = lanes(R)
        l0, l127 = lane == 0, lane == NB - 1

        def packed(f):
            return pzw[q, :] if f == 4 else pk[f, rows, :]

        def edge_east(f, x):
            return jnp.where(l127, roll(pk[f, rows, :], NB - 2 - L_EXTRA), roll(x, NB - 1))

        km = kd[0, rows, :]
        dm = kd[1, rows, :]
        ke, de = edge_east(0, km), edge_east(1, dm)
        kw = jnp.where(l0, roll(pk[0, rows, :], NB - L_EXTRA), roll(km, 1))
        the = de / jnp.maximum(ke, 1.0)
        nu = jnp.minimum(km, ke)
        nuw = jnp.minimum(km, kw)
        nv = jnp.minimum(km, kd[0, rows_n, :])
        nvs = jnp.minimum(km, kd[0, rows_s, :])
        faces[0, q, :] = nu
        faces[1, q, :] = nv

        for f in range(5):
            hb[0, f] = packed(f)
            hb[1, f] = roll(packed(f), NB - 2)

        def level(k, carry):
            ce, gus, gvs, du, dv, dt, ds = carry
            kf = k.astype(f32)
            kf1 = kf + 1.0
            u, un, us = xb[0, k, rows, :], xb[0, k, rows_n, :], xb[0, k, rows_s, :]
            v, vn, vs = xb[1, k, rows, :], xb[1, k, rows_n, :], xb[1, k, rows_s, :]

            slot_e, slot_w, slot_new = lax.rem(k + 1, 4), lax.rem(k, 4), lax.rem(k + 2, 4)

            def he(f, x):
                return jnp.where(l127, hb[slot_e, f], x)

            def hw(f, x):
                return jnp.where(l0, hb[slot_w, f], x)

            ue, uw = sh[0, k, q, :], sp[0, k, rows, :]
            ve, vw = sp[1, k, rows, :], sh[1, k, q, :]
            wsum = v + vs + he(4, ve + sp[1, k, rows_s, :])
            zsum = u + un + hw(4, uw + sp[0, k, rows_n, :])
            ue, uw, ve, vw = he(0, ue), hw(0, uw), he(1, ve), hw(1, vw)
            t, s = xb[2, k, rows, :], xb[3, k, rows, :]
            te, tw = he(2, sh[2, k, q, :]), hw(2, sh[3, k, q, :])
            se, sw = he(3, sh[4, k, q, :]), hw(3, sh[5, k, q, :])
            rho = jnp.where(kf < ke, BETA_S * se - ALPHA_T * te, 0.0)
            ce = ce + rho
            p = pb[k, rows, :]
            gu = p - (ce - 0.5 * rho) * the - (0.5 * u * (ue - uw) + (0.125 * wsum) * (un - us))
            gv = p - pb[k, rows_n, :] - ((0.125 * zsum) * (ve - vw) + 0.5 * v * (vn - vs))
            mu, mv = kf < nu, kf < nv
            gu = jnp.where(mu, gu, 0.0)
            gv = jnp.where(mv, gv, 0.0)
            inner, last = tab[0, k], tab[1, k]
            fu = jnp.where(kf1 < nu, inner, jnp.where(mu, last, 0.0))
            fv = jnp.where(kf1 < nv, inner, jnp.where(mv, last, 0.0))
            du = fu * (u + ADV_COURANT * gu + VISC_NUM * du)
            dv = fv * (v + ADV_COURANT * gv + VISC_NUM * dv)
            u2[k, q, :] = du
            v2[k, q, :] = dv
            u = jnp.where(mu, ADV_COURANT * u, 0.0)
            v = jnp.where(mv, ADV_COURANT * v, 0.0)
            uw = jnp.where(kf < nuw, ADV_COURANT * uw, 0.0)
            vs = jnp.where(kf < nvs, ADV_COURANT * vs, 0.0)
            um, vm = jnp.minimum(u, 0.0), jnp.minimum(v, 0.0)
            uwp, vsp = jnp.maximum(uw, 0.0), jnp.maximum(vs, 0.0)
            here = 1.0 - (((u - um) - (uw - uwp)) + ((v - vm) - (vs - vsp)))
            fc = jnp.where(kf1 < km, tab[3, k], jnp.where(kf < km, tab[4, k], 0.0))

            def tracer(i, x, xe, xw, d):
                moved = here * x + (uwp * xw - um * xe) + (vsp * xb[i, k, rows_s, :] - vm * xb[i, k, rows_n, :])
                return fc * (moved + DIFF_NUM * d)

            dt = tracer(2, t, te, tw, dt)
            ds = tracer(3, s, se, sw, ds)
            t2[k, q, :] = dt
            s2[k, q, :] = ds
            for f in range(5):
                hb[slot_new, f] = roll(packed(f), NB - 4 - 2 * k)
            return ce, gus + gu, gvs + gv, du, dv, dt, ds

        zero = jnp.zeros((R, NB), f32)
        _, gus, gvs, _, _, _, _ = levels(level, (zero,) * 7, 1)
        dn = kd[1, rows_n, :]
        hu = jnp.where(nu > 0, 0.5 * (dm + de), 0.0)
        hv = jnp.where(nv > 0, 0.5 * (dm + dn), 0.0)
        fx = hu * gus / jnp.maximum(nu, 1.0)
        fy = hv * gvs / jnp.maximum(nv, 1.0)
        wo[4, pl.ds(HW + c * R, R), :] = fx
        wo[5, pl.ds(HW + c * R, R), :] = fy
        wps[2, q, :] = pair(fx, fy)

    for c in range(CH):
        columns(c)
    for g in (g_c, g_n, g_s, d_n, d_s):
        g.each(["f"], start)

    def back(c):
        q = pl.ds(c * R, R)

        def level(i, carry):
            xu, xv, xt, xs, su, sv = carry
            k = LV - 1 - i
            ru, rc = tab[2, k], tab[5, k]
            xu = u2[k, q, :] + ru * xu
            xv = v2[k, q, :] + ru * xv
            xt = t2[k, q, :] + rc * xt
            xs = s2[k, q, :] + rc * xs
            u2[k, q, :] = xu
            v2[k, q, :] = xv
            t2[k, q, :] = xt
            s2[k, q, :] = xs
            return xu, xv, xt, xs, su + xu, sv + xv

        zero = jnp.zeros((R, NB), f32)
        out = levels(level, (zero,) * 6, 4)
        mean[0, q, :] = out[4] / jnp.maximum(faces[0, q, :], 1.0)
        mean[1, q, :] = out[5] / jnp.maximum(faces[1, q, :], 1.0)

    for c in range(CH):
        back(c)

    g_c.each(["w", "f"], wait_recv)
    from_s.each(["w", "f", ("d", "w"), ("d", "f")], wait_recv)
    from_n.each(["w", "f", ("d", "w"), ("d", "f")], wait_recv)

    ETA, U, V, WU, WV, PU, PV, WC = range(8)
    for i in range(8):
        for t in range(2):
            for r in (0, PAD + NW):
                bt[i, t, pl.ds(r, PAD), :] = jnp.zeros((PAD, NB), f32)

    def unpack(c, carry):
        src = pl.ds(pl.multiple_of(c * R, R), R)
        dst = pl.ds(pl.multiple_of(c * R + PAD, PAD), R)
        e1, u1 = unpair(wx[0, src, :])
        v1, d1 = unpair(wx[1, src, :])
        x1, y1 = unpair(wx[2, src, :])
        for t, (e, u, v, d, x, y) in enumerate((tuple(wo[i, src, :] for i in range(6)), (e1, u1, v1, d1, x1, y1))):
            bt[ETA, t, dst, :] = e
            bt[U, t, dst, :] = u
            bt[V, t, dst, :] = v
            bt[WC, t, dst, :] = d
            bt[PU, t, dst, :] = (ADV_COURANT / SUBCYCLES) * x
            bt[PV, t, dst, :] = (ADV_COURANT / SUBCYCLES) * y
        return carry
    lax.fori_loop(0, NW // R, unpack, 0)

    wchunks = [PAD + c * R for c in range(NW // R)]
    l0, l127 = lanes(R) == 0, lanes(R) == NB - 1
    for r in wchunks:
        rows = pl.ds(r, R)
        d = [bt[WC, t, rows, :] for t in range(2)]
        dn = [bt[WC, t, pl.ds(r + 1, R), :] for t in range(2)]
        for t in range(2):
            de = east(d[t], d[1 - t], l0)
            fu = (d[t] > 0) & (de > 0)
            fv = (d[t] > 0) & (dn[t] > 0)
            bt[WU, t, rows, :] = jnp.where(fu, WAVE_COURANT * (0.5 * (d[t] + de)), 0.0)
            bt[WV, t, rows, :] = jnp.where(fv, WAVE_COURANT * (0.5 * (d[t] + dn[t])), 0.0)
            bt[U, t, rows, :] = jnp.where(fu, bt[U, t, rows, :], 0.0)
            bt[V, t, rows, :] = jnp.where(fv, bt[V, t, rows, :], 0.0)
            bt[ETA, t, rows, :] = jnp.where(d[t] > 0, bt[ETA, t, rows, :], 0.0)
    for r in wchunks:
        for t in range(2):
            bt[WC, t, pl.ds(r, R), :] = jnp.where(bt[WC, t, pl.ds(r, R), :] > 0, WAVE_COURANT, 0.0)
    corr[...] = jnp.zeros((2, NB, NB), f32)

    def subcycle(n, carry):
        wn = tab[6, n]
        for r in wchunks:
            rows = pl.ds(r, R)
            uu = [bt[U, t, rows, :] for t in range(2)]
            for t in range(2):
                uw = west(uu[t], uu[1 - t], l127)
                div = uu[t] - uw + bt[V, t, rows, :] - bt[V, t, pl.ds(r - 1, R), :]
                bt[ETA, t, rows, :] = bt[ETA, t, rows, :] - bt[WC, t, rows, :] * div
        for i, r in enumerate(wchunks):
            rows = pl.ds(r, R)
            ee = [bt[ETA, t, rows, :] for t in range(2)]
            for t in range(2):
                xe = east(ee[t], ee[1 - t], l0)
                xn = bt[ETA, t, pl.ds(r + 1, R), :]
                un = bt[U, t, rows, :] - bt[WU, t, rows, :] * (xe - ee[t]) + bt[PU, t, rows, :]
                vn = bt[V, t, rows, :] - bt[WV, t, rows, :] * (xn - ee[t]) + bt[PV, t, rows, :]
                bt[U, t, rows, :] = un
                bt[V, t, rows, :] = vn
                if t == 0 and HW + PAD <= r < HW + PAD + NB:
                    q = pl.ds(r - HW - PAD, R)
                    corr[0, q, :] = corr[0, q, :] + wn * un
                    corr[1, q, :] = corr[1, q, :] + wn * vn
        return carry
    lax.fori_loop(0, SUBCYCLES, subcycle, 0)

    core = pl.ds(PAD + HW, NB)
    eta_o[...] = bt[ETA, 0, core, :]
    tu_o[...] = bt[U, 0, core, :]
    tv_o[...] = bt[V, 0, core, :]
    for i, w in ((0, WU), (1, WV)):
        depth = bt[w, 0, core, :] * (1.0 / WAVE_COURANT)
        corr[i] = corr[i] / jnp.where(depth > 0, depth, 1.0) - mean[i]

    g_c.each(list(g_c.copies), wait_send)
    for g in (g_n, g_s, d_n, d_s):
        g.each(list(g.copies), wait_send)


def finish_kernel(u2, v2, t2, s2, corr, faces, eta_r, tu_r, tv_r,
                  eta_o, tu_o, tv_o, uo_h, vo_h, to_h, so_h, out, tsem, osem):
    tracers = [pltpu.make_async_copy(src, dst, tsem.at[i]) for i, (src, dst) in enumerate(((t2, to_h), (s2, so_h)))]
    for copy in tracers:
        copy.start()
    eta_o[...] = eta_r[...]
    tu_o[...] = tu_r[...]
    tv_o[...] = tv_r[...]
    copies = []
    for c in range(CH):
        q = pl.ds(c * R, R)
        for i, (src, dst) in enumerate(((u2, uo_h), (v2, vo_h))):
            n, add = faces[i, q, :], corr[i, q, :]

            def level(k, carry):
                out[i, k, q, :] = src[k, q, :] + jnp.where(k.astype(f32) < n, add, 0.0)
                return carry
            levels(level, 0, 8)
            copy = pltpu.make_async_copy(out.at[i, :, q, :], dst.at[:, q, :], osem.at[i, c])
            copy.start()
            copies.append(copy)
    for copy in tracers + copies:
        copy.wait()


def solution(mesh):
    nrow = mesh.shape["row"]
    vm = pl.BlockSpec(memory_space=pltpu.VMEM)
    sm = pl.BlockSpec(memory_space=pltpu.SMEM)
    hb = pl.BlockSpec(memory_space=pltpu.HBM)
    table = solver_tables()

    def sds(*shape):
        return jax.ShapeDtypeStruct(shape, f32)

    def step(*args):
        args = [pltpu.with_memory_space_constraint(x, pltpu.HBM) for x in (jnp.asarray(table),) + args]
        outs = pl.pallas_call(
            functools.partial(main_kernel, nrow),
            out_shape=(sds(LV, NB, NB),) * 4 + (sds(2, NB, NB),) * 2 + (sds(NB, NB),) * 3,
            in_specs=[sm] + [hb] * 4 + [vm] * 5,
            out_specs=(vm,) * 9,
            scratch_shapes=[
                pltpu.VMEM((4, LV, NP, NB), f32),
                pltpu.VMEM((2, LV, NP, NB), f32),
                pltpu.VMEM((6, LV, NB, NB), f32),
                pltpu.VMEM((LV, NP, NB), f32),
                pltpu.VMEM((NB, NB), f32),
                pltpu.VMEM((4, 5, R, NB), f32),
                pltpu.VMEM((4, NP, NB), f32),
                pltpu.VMEM((4, NB, NB), f32),
                pltpu.VMEM((NB, NB), f32),
                pltpu.VMEM((2, NP, NB), f32),
                pltpu.VMEM((6, NW, NB), f32),
                pltpu.VMEM((3, NW, NB), f32),
                pltpu.VMEM((3, NB, NB), f32),
                pltpu.VMEM((8, 2, NWP, NB), f32),
                pltpu.VMEM((2, NB, NB), f32),
                pltpu.SemaphoreType.DMA((4,)),
                pltpu.SemaphoreType.DMA((29,)),
                pltpu.SemaphoreType.DMA((29,)),
            ],
            compiler_params=pltpu.CompilerParams(collective_id=0, has_side_effects=True, vmem_limit_bytes=41 * 2 ** 20),
            name="ocean",
        )(*args)
        return pl.pallas_call(
            finish_kernel,
            out_shape=(sds(NB, NB),) * 3 + (sds(LV, NB, NB),) * 4,
            in_specs=[vm] * 9,
            out_specs=(vm,) * 3 + (hb,) * 4,
            scratch_shapes=[
                pltpu.VMEM((2, LV, NB, NB), f32),
                pltpu.SemaphoreType.DMA((2,)),
                pltpu.SemaphoreType.DMA((2, CH)),
            ],
            compiler_params=pltpu.CompilerParams(vmem_limit_bytes=12 * 2 ** 20),
            name="finish",
        )(*outs)

    s3, s2 = P(None, "row", "col"), P("row", "col")
    return jax.shard_map(step, mesh=mesh, in_specs=(s3,) * 4 + (s2,) * 5,
                         out_specs=(s2,) * 3 + (s3,) * 4, check_vma=False)
```

time: 107 us -> 51.2 us (0.48)
  Pallas kernels: 93.9 us -> 50.4 us
  local copies, waits for them, and re-layouts: 11.9 us -> 0 us
    pallas_call x2, Pallas kernels: 93.9 us -> 50.4 us  [the longest x1 45.6 us: step(): pl.pallas_call(functools.partial(main_kernel, nrow), out_shape=(sds(LV, N...]
    unnamed x20 -> x0, local copies, waits for them, and re-layouts: 11.9 us -> none
where the time goes in v2:
time: 51.2 us; the launch traced here: 51 us
  Pallas kernels  50.4 us (98%)
  between operations  0.64 us (1%)
    pallas_call x1, Pallas kernels, step(): pl.pallas_call(functools.partial(main_kernel, nrow), out_shape=(sds(LV, N...  45.6 us
    pallas_call x1, Pallas kernels, step(): pl.pallas_call(finish_kernel, out_shape=(sds(NB, NB),) * 3 + (sds(LV, NB,...  4.78 us

profile of v2, /device:TPU:0, one launch (start us, length us, event | category | flops | bytes accessed | tf_op | source)
XLA Modules:
  0.0 51.0 jit_solution(17392231775669176873)
XLA Ops:
  0.6 45.6 %ocean.1 = (f32[41,128,128]{2,1,0:T(8,128)S(1)}, f32[41,128,128]{2,1,0:T(8,128)S(1)}, f32[41,128,128]{2,1,0:T(8,128)S(1)}, f32[41,128,128]{2,1,0:T(8,128)S(1)}, ...) custom-call(f32[8,128]{1,0:T(8,128)} %constant.2.clone.tab, ...), custom_call_target="tpu_custom_call" | custom-call | tf_op jit(solution)/shard_map/ocean/pallas_call | solution.py:547
  46.2 4.8 %finish.1 = (f32[128,128]{1,0:T(8,128)}, f32[128,128]{1,0:T(8,128)}, f32[128,128]{1,0:T(8,128)}, f32[41,128,128]{2,1,0:T(8,128)}, f32[41,128,128]{2,1,0:T(8,128)...) custom-call(f32[41,128,128]{2,1,0:T(8,128)S(1)} %get-tuple-element.16.u2, f32[41,128,128]{2,1,0:T(8,128)S(1)} %get-tuple-element.17.v2, ...), custom_call_target="tpu_custom_call" | custom-call | tf_op jit(solution)/shard_map/finish/pallas_call | solution.py:575
